TPU v7x, 128 devices: a whole 4x4x4 slice. The times are simulated.
128 devices in a mesh: dp: 32 (over x, z, core), tensor: 4 (over y).
Axes of the slice: x: 4, y: 4, z: 4, core: 2. Of those that a mesh axis runs over, the one named last changes fastest.
Arguments:
- tokens: bfloat16 [2, 2048, 4096], P(None, 'dp', 'tensor'), may hold values from -6 to 6
- routes: int32 [2, 2048, 2], P(None, 'dp'), may hold values from 0 to 7, all different within a row; in each aligned block of 64 rows (0 to 63, 64 to 127, ..., all dimensions but the last counted through in order) at most 20 rows name the same one
- probs: float32 [2, 2048, 8], P(None, 'dp'), may hold values from 0 to 1, as said below
- w_gate: bfloat16 [32, 4096, 3584], P('dp', None, 'tensor'), may hold values from -0.09375 to 0.09375
- w_up: bfloat16 [32, 4096, 3584], P('dp', None, 'tensor'), may hold values from -0.09375 to 0.09375
- w_down: bfloat16 [32, 3584, 4096], P('dp', 'tensor'), may hold values from -0.046875 to 0.046875
Outputs:
- mixed: bfloat16 [2, 2048, 4096], P(None, 'dp', 'tensor')
- aux_loss: float32 [2, 8], replicated
Inputs may be any that keep to these rules, and one draw needn't show every extreme that they name: `routes`: in each aligned block of 64 rows (the rows of one index of dp in one micro-batch) no expert is named in more than 20 entries; the 2 experts of a row differ. `probs`: each row is positive and sums to one.
All inputs are finite; a program needn't handle non-finite values.
Results may differ from a plain program's by a relative error of at most 0.012.
Values may be sent and summed in bfloat16 or wider, within the bound.
A program may use at most 128 MiB of HBM per device.

v0:
```python
import jax
import jax.numpy as jnp
from jax import lax
from jax.sharding import PartitionSpec as P

MICRO = 2
CAP = 20


def together(arrays, axis):
    ravelled, at, gathered = (jnp.concatenate([a.reshape(-1) for a in arrays]), 0, [])
    subtotal = lax.psum(ravelled, axis)
    for a in arrays:
        gathered.append(subtotal[at : at + a.size].reshape(a.shape))
        at += a.size
    return tuple(gathered)


def slot_tables(route, prob):
    rows_count = route.shape[0]
    experts = prob.shape[-1]
    capacity = CAP
    flat = route.reshape(-1)
    onehot = (flat[:, None] == jnp.arange(experts, dtype=jnp.int32)[None, :]).astype(jnp.int32)
    before = jnp.cumsum(onehot, axis=0) - onehot
    place = jnp.sum(before * onehot, axis=1)
    slot = flat * capacity + place
    picked = jnp.take_along_axis(prob, route, axis=1)
    weights = picked / jnp.sum(picked, axis=1, keepdims=True)
    grid = (slot[:, None] == jnp.arange(experts * capacity, dtype=jnp.int32)[None, :]).astype(
        jnp.float32
    )
    grid = grid.reshape(rows_count, route.shape[1], experts * capacity)
    dispatch = jnp.sum(grid, axis=1).T.astype(jnp.bfloat16)
    combine = jnp.sum(grid * weights[:, :, None], axis=1)
    counts = jnp.sum(onehot, axis=0).astype(jnp.float32)
    return (dispatch, combine, counts)


def spread_slots(slots, experts, copies_per, capacity):
    width = slots.shape[-1]
    wide = jnp.broadcast_to(
        slots.reshape(experts, 1, capacity, width), (experts, copies_per, capacity, width)
    )
    return wide.reshape(experts * copies_per, capacity, width)


def local(tokens, routes, probs, w_gate, w_up, w_down):
    groups = lax.axis_size("dp")
    experts = probs.shape[-1]
    copies_per = groups // experts
    capacity = CAP
    gate_local = w_gate[0]
    up_local = w_up[0]
    down_local = w_down[0]
    rows_local = tokens.shape[1]
    total_rows = rows_local * groups
    top_count = routes.shape[-1]
    tables = [slot_tables(routes[index], probs[index]) for index in range(MICRO)]
    prob_local = [jnp.sum(probs[index], axis=0) for index in range(MICRO)]
    count_table, prob_table = together(
        (jnp.stack([tables[index][2] for index in range(MICRO)]), jnp.stack(prob_local)), "dp"
    )
    outputs = []
    loss_terms = []
    for micro_index in range(MICRO):
        dispatch, combine, counts = tables[micro_index]
        count_all = count_table[micro_index]
        prob_all = prob_table[micro_index]
        width_local = tokens.shape[2]
        slots = jnp.dot(dispatch, tokens[micro_index], preferred_element_type=jnp.float32).astype(
            jnp.bfloat16
        )
        arrived = lax.all_to_all(
            spread_slots(slots, experts, copies_per, capacity),
            "dp",
            split_axis=0,
            concat_axis=0,
            tiled=True,
        )
        piece = lax.all_gather(arrived, "tensor", axis=2, tiled=True)
        piece_rows = piece.reshape(-1, piece.shape[2])
        gate = jnp.dot(piece_rows, gate_local, preferred_element_type=jnp.float32)
        up = jnp.dot(piece_rows, up_local, preferred_element_type=jnp.float32)
        hidden = (jax.nn.silu(gate) * up).astype(jnp.bfloat16)
        part = jnp.dot(hidden, down_local, preferred_element_type=jnp.float32).astype(jnp.bfloat16)
        reduced = lax.psum_scatter(part, "tensor", scatter_dimension=1, tiled=True).astype(
            jnp.float32
        )
        returned = lax.all_to_all(
            reduced.reshape(groups, capacity, width_local).astype(jnp.bfloat16),
            "dp",
            split_axis=0,
            concat_axis=0,
            tiled=True,
        ).astype(jnp.float32)
        summed = jnp.sum(returned.reshape(experts, copies_per, capacity, width_local), axis=1)
        mixed = jnp.dot(
            combine,
            summed.reshape(experts * capacity, width_local),
            precision=lax.Precision.HIGHEST,
            preferred_element_type=jnp.float32,
        )
        outputs.append(mixed.astype(jnp.bfloat16))
        loss_terms.append(
            experts * (count_all / (total_rows * top_count)) * (prob_all / total_rows)
        )
    return (jnp.stack(outputs), jnp.stack(loss_terms))


def solution(mesh):
    in_specs = (
        P(None, "dp", "tensor"),
        P(None, "dp", None),
        P(None, "dp", None),
        P("dp", None, "tensor"),
        P("dp", None, "tensor"),
        P("dp", "tensor", None),
    )
    out_specs = (P(None, "dp", "tensor"), P())
    return jax.shard_map(local, mesh=mesh, in_specs=in_specs, out_specs=out_specs, check_vma=False)
```

profile of v0, /device:TPU:1, one launch (start us, length us, event | category | flops | bytes accessed | tf_op | source)
XLA Modules:
  0.0 393.9 jit_solution(13326397115779215763)
XLA Ops:
  7.9 0.7 bitcast_or_fusion.1
  10.4 0.9 slice_reduce_fusion.1
  11.5 1.0 gather_fusion
  13.0 1.0 gather_fusion.1
  15.0 32.2 %all_to_all.20 = bf16[32,20,1024]{2,1,0:T(8,128)(2,1)} all-to-all(bf16[32,20,1024]{2,1,0:T(8,128)(2,1)S(1)} %bitcast.97), channel_id=1, replica_groups=mesh['dp'=32,'tensor'=4] {'dp'}, dimensions={0} | all-to-all | bytes 2621440 | tf_op jit(solution)/shard_map/all_to_all | solution.py:74
  47.8 26.4 %all_to_all.21 = bf16[32,20,1024]{2,1,0:T(8,128)(2,1)} all-to-all(bf16[32,20,1024]{2,1,0:T(8,128)(2,1)S(1)} %bitcast.98), channel_id=1, replica_groups=mesh['dp'=32,'tensor'=4] {'dp'}, dimensions={0} | all-to-all | bytes 2621440 | tf_op jit(solution)/shard_map/all_to_all | solution.py:74
  74.2 36.0 %all-gather.5.cloned.1.call-done = bf16[32,20,4096]{2,1,0:T(8,128)(2,1)} async-done(((bf16[32,20,1024]{2,1,0:T(8,128)(2,1)}), bf16[32,20,4096]{2,1,0:T(8,128)(2,1)}) %all-gather.5.cloned.1.call-update) | async-done | bytes 5242896 | tf_op jit(solution)/shard_map/all_gather | solution.py:81
  110.3 7.8 %reshape.140 = bf16[640,4096]{1,0:T(8,128)(2,1)} reshape(bf16[32,20,4096]{2,1,0:T(8,128)(2,1)} %all-gather.5.cloned.1.call-done) | data formatting | bytes 10485760 | tf_op jit(solution)/shard_map/reshape | solution.py:82
  118.0 11.7 %fusion.8 = f32[640,896]{1,0:T(8,128)S(1)} fusion(bf16[640,4096]{1,0:T(8,128)(2,1)} %reshape.140, bf16[1,4096,896]{2,1,0:T(8,128)(2,1)} %param.11), kind=kOutput, calls=%fused_computation.10 | convolution fusion | flops 4697620480 | bytes 14876672 | tf_op jit(solution)/shard_map/dot_general | solution.py:83
  129.7 18.9 %fusion.15 = bf16[640,4096]{1,0:T(8,128)(2,1)} fusion(bf16[1,896,4096]{2,1,0:T(8,128)(2,1)} %param.13, f32[640,896]{1,0:T(8,128)S(1)} %fusion.8, bf16[640,4096]{1,0:T(8,128)(2,1)} %reshape.140, bf16[1,4096,896]{2,1,0:T(8,128)(2,1)} %param.12), kind=kOutput, calls=%fused_computation.15 | convolution fusion | flops 9401303040 | bytes 27459584 | tf_op jit(solution)/shard_map/dot_general | solution.py:86
  148.8 29.4 %all-gather.3.cloned.1.call-done = bf16[32,20,4096]{2,1,0:T(8,128)(2,1)} async-done(((bf16[32,20,1024]{2,1,0:T(8,128)(2,1)}), bf16[32,20,4096]{2,1,0:T(8,128)(2,1)}) %all-gather.3.cloned.1.call-update) | async-done | bytes 5242896 | tf_op jit(solution)/shard_map/all_gather | solution.py:81
  178.2 7.7 %reshape.135 = bf16[640,4096]{1,0:T(8,128)(2,1)} reshape(bf16[32,20,4096]{2,1,0:T(8,128)(2,1)} %all-gather.3.cloned.1.call-done) | data formatting | bytes 10485760 | tf_op jit(solution)/shard_map/reshape | solution.py:82
  185.9 11.6 %fusion.10 = f32[640,896]{1,0:T(8,128)S(1)} fusion(bf16[640,4096]{1,0:T(8,128)(2,1)} %reshape.135, bf16[1,4096,896]{2,1,0:T(8,128)(2,1)} %param.11), kind=kOutput, calls=%fused_computation.12 | convolution fusion | flops 4697620480 | bytes 14876672 | tf_op jit(solution)/shard_map/dot_general | solution.py:83
  197.5 18.9 %fusion.12 = bf16[640,4096]{1,0:T(8,128)(2,1)} fusion(bf16[1,896,4096]{2,1,0:T(8,128)(2,1)} %param.13, f32[640,896]{1,0:T(8,128)S(1)} %fusion.10, bf16[640,4096]{1,0:T(8,128)(2,1)} %reshape.135, bf16[1,4096,896]{2,1,0:T(8,128)(2,1)} %param.12), kind=kOutput, calls=%fused_computation.14 | convolution fusion | flops 9401303040 | bytes 27459584 | tf_op jit(solution)/shard_map/dot_general | solution.py:86
  216.4 20.4 %reduce-scatter.5.cloned.1.call-done = bf16[640,1024]{1,0:T(8,128)(2,1)} async-done(((bf16[640,4096]{1,0:T(8,128)(2,1)}), bf16[640,1024]{1,0:T(8,128)(2,1)}) %reduce-scatter.5.cloned.1.call-update) | async-done | bytes 1310736 | tf_op jit(solution)/shard_map/reduce_scatter | solution.py:87
  236.8 3.2 convert_element_type.98
  240.0 7.7 %all-to-all-start.3 = ((bf16[32,20,1024]{2,1,0:T(8,128)(2,1)}), bf16[32,20,1024]{2,1,0:T(8,128)(2,1)S(1)}, u32[]{:S(2)}, u32[]{:S(2)}) async-start(bf16[32,20,1024]{2,1,0:T(8,128)(2,1)} %convert_element_type.98), calls=%async_computation.5 | async-start | bytes 3145728 | tf_op jit(solution)/shard_map/all_to_all | solution.py:90
  247.7 46.5 %reduce-scatter.3.cloned.1.call-done = bf16[640,1024]{1,0:T(8,128)(2,1)} async-done(((bf16[640,4096]{1,0:T(8,128)(2,1)}), bf16[640,1024]{1,0:T(8,128)(2,1)}) %reduce-scatter.3.cloned.1.call-update) | async-done | bytes 1310736 | tf_op jit(solution)/shard_map/reduce_scatter | solution.py:87
  294.3 3.2 convert_element_type.90
  297.5 7.7 %all-to-all-start.1 = ((bf16[32,20,1024]{2,1,0:T(8,128)(2,1)}), bf16[32,20,1024]{2,1,0:T(8,128)(2,1)S(1)}, u32[]{:S(2)}, u32[]{:S(2)}) async-start(bf16[32,20,1024]{2,1,0:T(8,128)(2,1)} %convert_element_type.90), calls=%async_computation.2 | async-start | bytes 3145728 | tf_op jit(solution)/shard_map/all_to_all | solution.py:90
  305.5 76.7 %psum.7 = f32[32]{0:T(128)S(1)} all-reduce(f32[32]{0:T(128)S(1)} %pad_maximum_fusion.4), channel_id=1, replica_groups=mesh['dp'=32,'tensor'=4] {'dp'}, use_global_device_ids=true, to_apply=%region_18.20 | all-reduce | flops 32 | bytes 256 | tf_op jit(solution)/shard_map/psum | solution.py:12
  382.9 1.2 convert_reduce_fusion
  384.0 1.2 reshape.143
  386.6 0.7 pad_maximum_fusion
  (60 shorter events, 7.3 us)
Async XLA Ops:
  7.2 103.1 %all-gather.5.cloned.1.call-start = ((), (), s32[]{:S(2)}) async-start(), calls=%async_computation.8 | async-start | bytes 7864320 | tf_op jit(solution)/shard_map/all_gather | solution.py:81
  13.0 1.3 copy-start.1
  13.0 1.5 copy-start
  47.2 131.0 %all-gather.3.cloned.1.call-start = ((), (), s32[]{:S(2)}) async-start(), calls=%async_computation.6 | async-start | bytes 7864320 | tf_op jit(solution)/shard_map/all_gather | solution.py:81
  74.2 162.6 %reduce-scatter.5.cloned.1.call-start = ((), (), s32[]{:S(2)}) async-start(), calls=%async_computation.9 | async-start | bytes 6553600 | tf_op jit(solution)/shard_map/reduce_scatter | solution.py:87
  148.6 145.7 %reduce-scatter.3.cloned.1.call-start = ((), (), s32[]{:S(2)}) async-start(), calls=%async_computation.7 | async-start | bytes 6553600 | tf_op jit(solution)/shard_map/reduce_scatter | solution.py:87
  240.0 57.5 %all-to-all-start.3 = ((bf16[32,20,1024]{2,1,0:T(8,128)(2,1)}), bf16[32,20,1024]{2,1,0:T(8,128)(2,1)S(1)}, u32[]{:S(2)}, u32[]{:S(2)}) async-start(bf16[32,20,1024]{2,1,0:T(8,128)(2,1)} %convert_element_type.98), calls=%async_computation.5 | async-start | bytes 3145728 | tf_op jit(solution)/shard_map/all_to_all | solution.py:90
  297.5 87.7 %all-to-all-start.1 = ((bf16[32,20,1024]{2,1,0:T(8,128)(2,1)}), bf16[32,20,1024]{2,1,0:T(8,128)(2,1)S(1)}, u32[]{:S(2)}, u32[]{:S(2)}) async-start(bf16[32,20,1024]{2,1,0:T(8,128)(2,1)} %convert_element_type.90), calls=%async_computation.2 | async-start | bytes 3145728 | tf_op jit(solution)/shard_map/all_to_all | solution.py:90
Sparse Core Ops, SparseCore 0:
  47.3 62.8 all-gather.4
  111.9 66.2 all-gather.2
  180.6 56.1 reduce-scatter.4
  239.1 55.1 reduce-scatter.2
where the time goes:
time: 395 us; the launch traced here: 394 us
  blocking collectives  135 us (34%)
  waiting for transfers between devices  132 us (33%)
  matrix products  62.5 us (16%)
  local copies, waits for them, and re-layouts  28.3 us (7%)
  starting transfers between devices  15.8 us (4%)
  between operations  14 us (4%)
  other arithmetic  5.56 us (1%)
    psum x1, blocking collectives, together(): subtotal = lax.psum(ravelled, axis)  76.7 us
    reduce_scatter x2, waiting for transfers between devices, local(): lax.psum_scatter(part, 'tensor', scatter_dimension=1, tiled=True)  67 us
    all_gather x2, waiting for transfers between devices, local(): piece = lax.all_gather(arrived, 'tensor', axis=2, tiled=True)  65.4 us
    all_to_all x2, blocking collectives, local(): lax.all_to_all(spread_slots(slots, experts, copies_per, capacity), 'dp',...  58.5 us
    dot_general x2, matrix products, local(): jnp.dot(hidden, down_local, preferred_element_type=jnp.float32)  37.8 us
    dot_general x2, matrix products, local(): gate = jnp.dot(piece_rows, gate_local, preferred_element_type=jnp.float32)  23.2 us
    all_to_all x2, starting transfers between devices, local(): lax.all_to_all(reduced.reshape(groups, capacity, width_local).astype(jnp....  15.4 us
    reshape x2, local copies, waits for them, and re-layouts, local(): piece_rows = piece.reshape(-1, piece.shape[2])  15.4 us
  transfers between devices with their start and end apart: 6, of which 4 were waited for; matrix products, arithmetic and copies ran while one was open for 22% of the time, Pallas kernels for 0%

commit v1 on v0

v1 whole, which is shorter than its diff:
```python
import jax
import jax.numpy as jnp
from jax import lax
from jax.experimental import pallas as pl
from jax.experimental.pallas import tpu as pltpu
from jax.sharding import PartitionSpec as P

MICRO = 2
CAP = 20
EXPERTS = 8
D = 4096
QUART = 1024
FFD = 896
ROWS = 80
HALF = 160
FULL = 320
SHIFTS = (0, 1, 3, 2)
NT = FFD // 128
MESH = pl.DeviceIdType.MESH
F32 = jnp.float32
BF16 = jnp.bfloat16


class Sems:
    def __init__(self):
        self.names = {}

    def __call__(self, *name):
        return self.names.setdefault(name, len(self.names))


N_SEND = 160
N_RECV = 160


def moe_kernel(
    tok_ref, meta_ref, wg_ref, wu_ref, wd_ref, out_ref, aux_ref,
    wgu, wdn, X, H, S, tok2, meta2, acc, R, DS, DR, OWN, T1, T2, T3, RR1, RR2, fin_in,
    stat_out, stat_in, stat_pair,
    wsem, ssem, rsem,
):
    dp = lax.axis_index("dp")
    y = lax.axis_index("tensor")
    x = dp // 8
    z = (dp // 2) % 4
    c = dp % 2
    zb = z % 2
    zh = z // 2

    def at(xx, zz, cc):
        return (xx * 8 + zz * 2 + cc, y)

    up = (dp, (y + 1) % 4)
    dn = (dp, (y + 3) % 4)
    partner = at(x, z, 1 - c)
    dests = [[at((x + 4 - s) % 4, 2 * c + i, 1 - zh) for i in range(2)] for s in SHIFTS]
    sources = [[at((x + s) % 4, 2 * (1 - c) + b, zh) for b in range(2)] for s in SHIFTS]

    send_ids, recv_ids = Sems(), Sems()
    pending = {}

    def msg(src, dst, dev, recv, offset=0):
        return pltpu.make_async_remote_copy(
            src_ref=src, dst_ref=dst, send_sem=None, recv_sem=rsem.at[recv + offset],
            device_id=dev, device_id_type=MESH,
        )

    def send(name, src, dst, dev, recv):
        copy = pltpu.make_async_remote_copy(
            src_ref=src, dst_ref=dst, send_sem=ssem.at[send_ids(*name)], recv_sem=rsem.at[recv],
            device_id=dev, device_id_type=MESH,
        )
        copy.start()
        pending[name] = copy

    def sent(*name):
        if name in pending:
            pending.pop(name).wait_send()

    def arrived(dst, recv):
        pltpu.make_async_remote_copy(
            src_ref=dst, dst_ref=dst, send_sem=ssem.at[0], recv_sem=rsem.at[recv],
            device_id=partner, device_id_type=MESH,
        ).wait_recv()

    P1 = [[recv_ids("p1", k, b) for b in range(2)] for k in range(4)]
    ST = [recv_ids("st", i) for i in range(8)]
    P3 = [[recv_ids("p3", k, i) for i in range(2)] for k in range(4)]

    barrier = pltpu.get_barrier_semaphore()
    greeted = [up, dn, partner]
    for k in range(4):
        greeted += dests[k] + sources[k]
    for dev in greeted:
        pl.semaphore_signal(barrier, inc=1, device_id=dev, device_id_type=MESH)

    wcopies = []
    for n in range(NT):
        cols = pl.ds(n * 128, 128)
        wcopies.append([
            pltpu.make_async_copy(wg_ref.at[:, cols], wgu.at[n, :, pl.ds(0, 128)], wsem.at[2 * n]),
            pltpu.make_async_copy(wu_ref.at[:, cols], wgu.at[n, :, pl.ds(128, 128)], wsem.at[2 * n + 1]),
        ])
    dcopy = pltpu.make_async_copy(wd_ref, wdn, wsem.at[2 * NT])
    for pair in wcopies:
        for copy in pair:
            copy.start()
    dcopy.start()

    meta2[0:128, :] = meta_ref[...]
    tok2[0:128, :] = tok_ref[...]
    pl.semaphore_wait(barrier, len(greeted))

    send(("meta",), meta_ref, meta2.at[pl.ds(128, 128)], partner, recv_ids("meta"))
    send(("tok",), tok_ref, tok2.at[pl.ds(128, 128)], partner, recv_ids("tok"))

    rid = lax.broadcasted_iota(jnp.int32, (256, 256), 0)
    cid = lax.broadcasted_iota(jnp.int32, (256, 256), 1)
    lower = jnp.where((rid // 64 == cid // 64) & (rid > cid), 1.0, 0.0).astype(BF16)
    arrived(meta2.at[pl.ds(128, 128)], recv_ids("meta"))
    meta = meta2[...]
    lane = lax.broadcasted_iota(jnp.int32, (256, 128), 1).astype(F32)
    r0, r1 = meta[:, 8:9], meta[:, 9:10]
    oh0 = jnp.where(lane == r0, 1.0, 0.0)
    oh1 = jnp.where(lane == r1, 1.0, 0.0)
    both = oh0 + oh1
    before = jnp.dot(lower, both.astype(BF16), preferred_element_type=F32)
    place0 = jnp.sum(before * oh0, axis=1, keepdims=True)
    place1 = jnp.sum(before * oh1, axis=1, keepdims=True)
    p0 = jnp.sum(meta * oh0, axis=1, keepdims=True)
    p1 = jnp.sum(meta * oh1, axis=1, keepdims=True)
    w0 = p0 / (p0 + p1)
    w1 = p1 / (p0 + p1)
    base = ((lax.broadcasted_iota(jnp.int32, (256, 1), 0) // 64) * CAP).astype(F32)
    s0 = base + place0
    s1 = base + place1

    def columns(k):
        e = (2 * ((x + 4 - SHIFTS[k]) % 4) + c).astype(F32)
        return jnp.where(r0 == e, s0, -1.0), jnp.where(r1 == e, s1, -1.0)

    def two_rows(v):
        a = jnp.sum(v[0:64] , axis=0, keepdims=True) + jnp.sum(v[128:192], axis=0, keepdims=True)
        b = jnp.sum(v[64:128], axis=0, keepdims=True) + jnp.sum(v[192:256], axis=0, keepdims=True)
        return a, b

    ca, cb = two_rows(both)
    pa, pb = two_rows(meta)
    stat_out[...] = jnp.concatenate([ca, cb, pa, pb, jnp.zeros((4, 128), F32)], axis=0)

    arrived(tok2.at[pl.ds(128, 128)], recv_ids("tok"))
    slot_lane = lax.broadcasted_iota(jnp.int32, (256, ROWS), 1).astype(F32)
    for k in range(4):
        c0, c1 = columns(k)
        place = (jnp.where(slot_lane == c0, 1.0, 0.0) + jnp.where(slot_lane == c1, 1.0, 0.0)).astype(BF16)
        S[k] = lax.dot_general(
            place, tok2[...], (((0,), (0,)), ((), ())), preferred_element_type=F32
        ).astype(BF16)
        for i in range(2):
            send(("p1", k, i), S.at[k], X.at[k, 0, pl.ds(pl.multiple_of(zb * ROWS, 16), ROWS)],
                 dests[k][i], P1[k][0] + zb)
            send(("st", k, i), stat_out, stat_in.at[x * 2 + zb], dests[k][i], ST[0] + x * 2 + zb)

    own = lambda b: pl.ds(b * ROWS, ROWS)
    other = lambda b: pl.ds(HALF + b * ROWS, ROWS)

    def to_partner(k, r, b):
        send(("d", k, r, b), X.at[k, r, own(b)], X.at[k, r, other(b)], partner, recv_ids("d", k, r, b))

    def gather_start(k):
        for b in range(2):
            arrived(X.at[k, 0, own(b)], P1[k][b])
            send(("u", k, b), X.at[k, 0, own(b)], X.at[k, 3, own(b)], up, recv_ids("u", k, b))
            send(("n", k, b), X.at[k, 0, own(b)], X.at[k, 1, own(b)], dn, recv_ids("n", k, b))
            to_partner(k, 0, b)

    def gather_forward(k):
        arrived(X.at[k, 3, own(0)], recv_ids("u", k, 0))
        send(("fu", k), X.at[k, 3, own(0)], X.at[k, 2, own(0)], up, recv_ids("fu", k))
        to_partner(k, 3, 0)
        arrived(X.at[k, 1, own(0)], recv_ids("n", k, 0))
        to_partner(k, 1, 0)
        arrived(X.at[k, 1, own(1)], recv_ids("n", k, 1))
        send(("fn", k), X.at[k, 1, own(1)], X.at[k, 2, own(1)], dn, recv_ids("fn", k))
        to_partner(k, 1, 1)
        arrived(X.at[k, 3, own(1)], recv_ids("u", k, 1))
        to_partner(k, 3, 1)

    def gather_end(k):
        arrived(X.at[k, 2, own(0)], recv_ids("fu", k))
        to_partner(k, 2, 0)
        arrived(X.at[k, 2, own(1)], recv_ids("fn", k))
        to_partner(k, 2, 1)

    def gathered(k):
        for r in (0, 3, 1, 2):
            for b in range(2):
                arrived(X.at[k, r, other(b)], recv_ids("d", k, r, b))

    def hidden(k, start, stop):
        def step(n, carry):
            total = None
            for r in range(4):
                rows = pl.ds(pl.multiple_of(((y + r) % 4) * QUART, QUART), QUART)
                term = jnp.dot(X[k, r], wgu[n, rows, :], preferred_element_type=F32)
                total = term if total is None else total + term
            gate, up_ = total[:, :128], total[:, 128:]
            value = gate / (1.0 + jnp.exp(-gate)) * up_
            H[:, pl.ds(pl.multiple_of(n * 128, 128), 128)] = value.astype(BF16)
            return carry

        if k == 0:
            for n in range(start, stop):
                for copy in wcopies[n]:
                    copy.wait()
        lax.fori_loop(start, stop, step, 0)

    def down(k):
        slot = k % 2
        if k == 0:
            dcopy.wait()
        for r in range(4):
            sent("ds", k - 2, r)

        def step(i, carry):
            r = 2 - i
            r = jnp.where(r < 0, 3, r)
            cols = pl.ds(pl.multiple_of(((y + r) % 4) * QUART, QUART), QUART)
            part = jnp.dot(H[...], wdn[:, cols], preferred_element_type=F32)
            OWN[slot, r] = part[:HALF]
            DS[slot, r] = part[HALF:].astype(BF16)
            return carry

        lax.fori_loop(0, 4, step, 0)
        for r in (2, 1, 3, 0):
            send(("ds", k, r), DS.at[slot, r], DR.at[k, r], partner, recv_ids("ds", k, r))

    def chip_sum(k, r):
        arrived(DR.at[k, r], recv_ids("ds", k, r))
        return OWN[k % 2, r] + DR[k, r].astype(F32)

    def scatter_start(k):
        slot = k % 2
        sent("a1", k - 2)
        sent("b1", k - 2)
        T1[slot] = chip_sum(k, 2).astype(BF16)
        send(("a1", k), T1.at[slot, pl.ds(0, ROWS)], RR1.at[k, 0], dn, recv_ids("a1", k))
        send(("b1", k), T1.at[slot, pl.ds(ROWS, ROWS)], RR1.at[k, 1], up, recv_ids("b1", k))

    def scatter_forward(k):
        slot = k % 2
        sent("a2", k - 2)
        sent("b2", k - 2)
        total = chip_sum(k, 3)
        arrived(RR1.at[k, 0], recv_ids("a1", k))
        T2[slot, 0, 0:ROWS] = (total[:ROWS] + RR1[k, 0].astype(F32)).astype(BF16)
        T2[slot, 0, ROWS:HALF] = total[ROWS:].astype(BF16)
        send(("a2", k), T2.at[slot, 0], RR2.at[k, 0], dn, recv_ids("a2", k))
        total = chip_sum(k, 1)
        arrived(RR1.at[k, 1], recv_ids("b1", k))
        T2[slot, 1, 0:ROWS] = total[:ROWS].astype(BF16)
        T2[slot, 1, ROWS:HALF] = (total[ROWS:] + RR1[k, 1].astype(F32)).astype(BF16)
        send(("b2", k), T2.at[slot, 1], RR2.at[k, 1], up, recv_ids("b2", k))

    def scatter_end(k):
        slot = k % 2
        for b in range(2):
            sent("p3", k - 2, b)
        total = chip_sum(k, 0)
        arrived(RR2.at[k, 0], recv_ids("a2", k))
        arrived(RR2.at[k, 1], recv_ids("b2", k))
        T3[slot] = (total + RR2[k, 0].astype(F32) + RR2[k, 1].astype(F32)).astype(BF16)
        for b in range(2):
            send(("p3", k, b), T3.at[slot, own(b)], R.at[k, pl.ds(pl.multiple_of(zb * ROWS, 16), ROWS)],
                 sources[k][b], P3[k][0] + zb)

    two_lane = lax.broadcasted_iota(jnp.int32, (256, HALF), 1)
    two_lane = jnp.where(two_lane >= ROWS, two_lane - ROWS, two_lane).astype(F32)

    def combine(k):
        for i in range(2):
            arrived(R.at[k, own(i)], P3[k][i])
        c0, c1 = columns(k)
        weight = jnp.where(two_lane == c0, w0, 0.0) + jnp.where(two_lane == c1, w1, 0.0)
        high = weight.astype(BF16)
        low = (weight - high.astype(F32)).astype(BF16)
        rows = R[k]
        term = jnp.dot(high, rows, preferred_element_type=F32) + jnp.dot(
            low, rows, preferred_element_type=F32
        )
        acc[...] = term if k == 0 else acc[...] + term

    gather_start(0)
    gather_start(1)
    gather_forward(0)
    gather_start(2)
    gather_end(0)
    for i in range(8):
        arrived(stat_in.at[i], ST[i])
    total = stat_in[0]
    for i in range(1, 8):
        total = total + stat_in[i]
    stat_pair[0] = total
    send(("sp",), stat_pair.at[0], stat_pair.at[1], partner, recv_ids("sp"))
    gathered(0)

    hidden(0, 0, 4)
    gather_forward(1)
    gather_start(3)
    hidden(0, 4, NT)
    gather_end(1)
    down(0)
    gathered(1)

    hidden(1, 0, 4)
    scatter_start(0)
    gather_forward(2)
    hidden(1, 4, NT)
    gather_end(2)
    scatter_forward(0)
    down(1)
    gathered(2)

    hidden(2, 0, 4)
    scatter_end(0)
    scatter_start(1)
    gather_forward(3)
    hidden(2, 4, NT)
    scatter_forward(1)
    gather_end(3)
    down(2)
    gathered(3)

    hidden(3, 0, 4)
    scatter_end(1)
    scatter_start(2)
    hidden(3, 4, NT)
    scatter_forward(2)
    combine(0)
    down(3)

    scatter_start(3)
    scatter_end(2)
    combine(1)
    scatter_forward(3)
    arrived(stat_pair.at[1], recv_ids("sp"))
    total = stat_pair[0] + stat_pair[1]
    aux_ref[...] = EXPERTS * (total[0:2, 0:8] / 4096.0) * (total[2:4, 0:8] / 2048.0)
    combine(2)
    scatter_end(3)
    combine(3)
    send(("fin",), acc.at[pl.ds(128, 128)], fin_in, partner, recv_ids("fin"))
    arrived(fin_in, recv_ids("fin"))
    out_ref[...] = (acc[0:128, :] + fin_in[...]).astype(BF16)
    for name in list(pending):
        sent(*name)
    assert len(send_ids.names) <= N_SEND and len(recv_ids.names) <= N_RECV


def local(tokens, routes, probs, w_gate, w_up, w_down):
    meta = jnp.concatenate(
        [probs.reshape(128, EXPERTS), routes.reshape(128, 2).astype(F32), jnp.zeros((128, 118), F32)], axis=1
    )
    vmem = pl.BlockSpec(memory_space=pltpu.VMEM)
    hbm = pl.BlockSpec(memory_space=pl.ANY)
    mixed, aux = pl.pallas_call(
        moe_kernel,
        out_shape=(jax.ShapeDtypeStruct((128, QUART), BF16), jax.ShapeDtypeStruct((2, 8), F32)),
        in_specs=[vmem, vmem, hbm, hbm, hbm],
        out_specs=(vmem, vmem),
        scratch_shapes=[
            pltpu.VMEM((NT, D, 256), BF16),
            pltpu.VMEM((FFD, D), BF16),
            pltpu.VMEM((4, 4, FULL, QUART), BF16),
            pltpu.VMEM((FULL, FFD), BF16),
            pltpu.VMEM((4, ROWS, QUART), BF16),
            pltpu.VMEM((256, QUART), BF16),
            pltpu.VMEM((256, 128), F32),
            pltpu.VMEM((256, QUART), F32),
            pltpu.VMEM((4, HALF, QUART), BF16),
            pltpu.VMEM((2, 4, HALF, QUART), BF16),
            pltpu.VMEM((4, 4, HALF, QUART), BF16),
            pltpu.VMEM((2, 4, HALF, QUART), F32),
            pltpu.VMEM((2, HALF, QUART), BF16),
            pltpu.VMEM((2, 2, HALF, QUART), BF16),
            pltpu.VMEM((2, HALF, QUART), BF16),
            pltpu.VMEM((4, 2, ROWS, QUART), BF16),
            pltpu.VMEM((4, 2, HALF, QUART), BF16),
            pltpu.VMEM((128, QUART), F32),
            pltpu.VMEM((8, 128), F32),
            pltpu.VMEM((8, 8, 128), F32),
            pltpu.VMEM((2, 8, 128), F32),
            pltpu.SemaphoreType.DMA((2 * NT + 1,)),
            pltpu.SemaphoreType.DMA((N_SEND,)),
            pltpu.SemaphoreType.DMA((N_RECV,)),
        ],
        compiler_params=pltpu.CompilerParams(
            collective_id=0, has_side_effects=True, vmem_limit_bytes=66_000_000
        ),
        name="moe",
    )(tokens.reshape(128, QUART), meta, w_gate[0], w_up[0], w_down[0])
    return mixed.reshape(MICRO, 64, QUART), aux


def solution(mesh):
    in_specs = (
        P(None, "dp", "tensor"),
        P(None, "dp", None),
        P(None, "dp", None),
        P("dp", None, "tensor"),
        P("dp", None, "tensor"),
        P("dp", "tensor", None),
    )
    out_specs = (P(None, "dp", "tensor"), P())
    return jax.shard_map(local, mesh=mesh, in_specs=in_specs, out_specs=out_specs, check_vma=False)
```

time: 395 us -> 147 us (0.37)
  Pallas kernels: 0 us -> 139 us
  blocking collectives: 135 us -> 0 us
  waiting for transfers between devices: 132 us -> 0 us
  matrix products: 62.5 us -> 0 us
  local copies, waits for them, and re-layouts: 28.3 us -> 3.87 us
  starting transfers between devices: 15.8 us -> 0 us
  between operations: 14 us -> 0.66 us
  other arithmetic: 5.56 us -> 1.41 us
    pallas_call x0 -> x1, Pallas kernels: none -> 139 us  [local(): pl.pallas_call(moe_kernel, out_shape=(jax.ShapeDtypeStruct((128, QUART),...]
    psum x1 -> x0, blocking collectives: 76.7 us -> none  [together(): subtotal = lax.psum(ravelled, axis)]
    reduce_scatter x2 -> x0, waiting for transfers between devices: 67 us -> none  [local(): lax.psum_scatter(part, 'tensor', scatter_dimension=1, tiled=True)]
    all_gather x2 -> x0, waiting for transfers between devices: 65.4 us -> none  [local(): piece = lax.all_gather(arrived, 'tensor', axis=2, tiled=True)]
    dot_general x8 -> x0, matrix products: 62.5 us -> none  [the longest x2 37.8 us: local(): jnp.dot(hidden, down_local, preferred_element_type=jnp.float32)]
    all_to_all x2 -> x0, blocking collectives: 58.5 us -> none  [local(): lax.all_to_all(spread_slots(slots, experts, copies_per, capacity), 'dp',...]
    reshape x6 -> x0, local copies, waits for them, and re-layouts: 16.9 us -> none  [the longest x2 15.4 us: local(): piece_rows = piece.reshape(-1, piece.shape[2])]
    all_to_all x2 -> x0, starting transfers between devices: 15.4 us -> none  [local(): lax.all_to_all(reduced.reshape(groups, capacity, width_local).astype(jnp....]
  transfers between devices with their start and end apart: 6 -> 0, of which waited for: 4 -> 0; matrix products, arithmetic and copies ran while one was open for 22% -> 0% of each run, Pallas kernels for 0% -> 0%
where the time goes in v1:
time: 147 us; the launch traced here: 145 us
  Pallas kernels  139 us (95%)
  local copies, waits for them, and re-layouts  3.87 us (3%)
    pallas_call x1, Pallas kernels, local(): pl.pallas_call(moe_kernel, out_shape=(jax.ShapeDtypeStruct((128, QUART),...  139 us
    unnamed x3, local copies, waits for them, and re-layouts  3.69 us

profile of v1, /device:TPU:1, one launch (start us, length us, event | category | flops | bytes accessed | tf_op | source)
XLA Modules:
  0.0 144.6 jit_solution(14918810088379631157)
XLA Ops:
  0.6 0.1 pad.2.clone
  0.7 0.7 convert_element_type.6
  1.4 0.1 copy.9
  1.5 0.8 copy.8
  2.3 0.7 maximum_maximum_fusion.meta_ref
  3.0 138.7 %moe.1 = (bf16[128,1024]{1,0:T(8,128)(2,1)}, f32[2,8]{1,0:T(2,128)}) custom-call(bf16[128,1024]{1,0:T(8,128)(2,1)} %bitcast.10, f32[128,128]{1,0:T(8,128)} %maximum_maximum_fusion.meta_ref, bf16[4096,896]{1,0:T(8,128)(2,1)} %bitcast.7, bf16[4096,896]{1,0:T(8,128)(2,1)} %bitcast.8, bf16[896,4096]{1,0:T(8,128)(2,1)} %bitcast.9), custom_call_target="tpu_custom_call" | custom-call | tf_op jit(solution)/shard_map/moe/pallas_call | solution.py:366
  141.7 1.7 %copy.12 = bf16[2,64,1024]{2,1,0:T(8,128)(2,1)} copy(bf16[2,64,1024]{2,1,0:T(8,128)(2,1)} %bitcast.13) | data formatting | bytes 524288
  143.4 1.2 copy.13
  (1 shorter events, 0.0 us)

commit v2 on v1

--- a/solution.py
+++ b/solution.py
@@ -14,7 +14,9 @@
 ROWS = 80
 HALF = 160
 FULL = 320
-SHIFTS = (0, 1, 3, 2)
+WT = 256
+WS = QUART - WT
+SHIFTS = (1, 3, 2, 0)
 NT = FFD // 128
 MESH = pl.DeviceIdType.MESH
 F32 = jnp.float32
@@ -29,13 +31,14 @@
         return self.names.setdefault(name, len(self.names))
 
 
-N_SEND = 160
-N_RECV = 160
+N_SEND = 200
+N_RECV = 200
 
 
 def moe_kernel(
     tok_ref, meta_ref, wg_ref, wu_ref, wd_ref, out_ref, aux_ref,
-    wgu, wdn, X, H, S, tok2, meta2, acc, R, DS, DR, OWN, T1, T2, T3, RR1, RR2, fin_in,
+    wgu, wdn, X, H, S, TS, tok2, tokT, PL, meta2, acc, accT, R, RT, DS, DR, OWN, T1, T2, T3, T4, RR1, RR2,
+    fin_in, finT_in, YS, YR,
     stat_out, stat_in, stat_pair,
     wsem, ssem, rsem,
 ):
@@ -52,6 +55,8 @@
 
     up = (dp, (y + 1) % 4)
     dn = (dp, (y + 3) % 4)
+    far = (dp, (y + 2) % 4)
+    round_y = {1: up, 2: far, 3: dn}
     partner = at(x, z, 1 - c)
     dests = [[at((x + 4 - s) % 4, 2 * c + i, 1 - zh) for i in range(2)] for s in SHIFTS]
     sources = [[at((x + s) % 4, 2 * (1 - c) + b, zh) for b in range(2)] for s in SHIFTS]
@@ -86,9 +91,11 @@
     P1 = [[recv_ids("p1", k, b) for b in range(2)] for k in range(4)]
     ST = [recv_ids("st", i) for i in range(8)]
     P3 = [[recv_ids("p3", k, i) for i in range(2)] for k in range(4)]
+    P1T = [[recv_ids("p1t", k, b) for b in range(2)] for k in range(4)]
+    P3T = [[recv_ids("p3t", k, i) for i in range(2)] for k in range(4)]
 
     barrier = pltpu.get_barrier_semaphore()
-    greeted = [up, dn, partner]
+    greeted = [up, dn, far, partner]
     for k in range(4):
         greeted += dests[k] + sources[k]
     for dev in greeted:
@@ -113,6 +120,11 @@
 
     send(("meta",), meta_ref, meta2.at[pl.ds(128, 128)], partner, recv_ids("meta"))
     send(("tok",), tok_ref, tok2.at[pl.ds(128, 128)], partner, recv_ids("tok"))
+    tcols = pl.ds(WS, WT)
+    scols = pl.ds(0, WS)
+    mine, theirs = pl.ds(0, 128), pl.ds(128, 128)
+    for r in (1, 3, 2):
+        send(("ty", r), tok_ref.at[:, tcols], tokT.at[4 - r, mine], round_y[r], recv_ids("ty", 4 - r))
 
     rid = lax.broadcasted_iota(jnp.int32, (256, 256), 0)
     cid = lax.broadcasted_iota(jnp.int32, (256, 256), 1)
@@ -150,55 +162,87 @@
 
     arrived(tok2.at[pl.ds(128, 128)], recv_ids("tok"))
     slot_lane = lax.broadcasted_iota(jnp.int32, (256, ROWS), 1).astype(F32)
-    for k in range(4):
+    block = pl.ds(pl.multiple_of(zb * ROWS, 16), ROWS)
+
+    def slots(k, rows):
+        return lax.dot_general(
+            PL[k], rows, (((0,), (0,)), ((), ())), preferred_element_type=F32
+        ).astype(BF16)
+
+    def dispatch(k):
         c0, c1 = columns(k)
-        place = (jnp.where(slot_lane == c0, 1.0, 0.0) + jnp.where(slot_lane == c1, 1.0, 0.0)).astype(BF16)
-        S[k] = lax.dot_general(
-            place, tok2[...], (((0,), (0,)), ((), ())), preferred_element_type=F32
-        ).astype(BF16)
+        PL[k] = (jnp.where(slot_lane == c0, 1.0, 0.0) + jnp.where(slot_lane == c1, 1.0, 0.0)).astype(BF16)
+        S[k] = slots(k, tok2[:, 0:WS])
         for i in range(2):
-            send(("p1", k, i), S.at[k], X.at[k, 0, pl.ds(pl.multiple_of(zb * ROWS, 16), ROWS)],
-                 dests[k][i], P1[k][0] + zb)
-            send(("st", k, i), stat_out, stat_in.at[x * 2 + zb], dests[k][i], ST[0] + x * 2 + zb)
+            send(("p1", k, i), S.at[k], X.at[k, 0, block, scols], dests[k][i], P1[k][0] + zb)
+
+    def tokens_along_y():
+        for r in (1, 3, 2):
+            arrived(tokT.at[r, mine], recv_ids("ty", r))
+            send(("td", r), tokT.at[r, mine], tokT.at[r, theirs], partner, recv_ids("td", r))
+        for r in (1, 3, 2):
+            arrived(tokT.at[r, theirs], recv_ids("td", r))
+
+    def dispatch_direct(k):
+        TS[k, 0] = slots(k, tok2[:, WS:QUART])
+        for r in range(1, 4):
+            TS[k, r] = slots(k, tokT[r])
+        for i in range(2):
+            send(("p1t", k, i), TS.at[k], X.at[k, :, block, tcols], dests[k][i], P1T[k][0] + zb)
+
+    def dispatch_stats():
+        for k in range(4):
+            for i in range(2):
+                send(("st", k, i), stat_out, stat_in.at[x * 2 + zb], dests[k][i], ST[0] + x * 2 + zb)
 
     own = lambda b: pl.ds(b * ROWS, ROWS)
     other = lambda b: pl.ds(HALF + b * ROWS, ROWS)
 
     def to_partner(k, r, b):
-        send(("d", k, r, b), X.at[k, r, own(b)], X.at[k, r, other(b)], partner, recv_ids("d", k, r, b))
+        send(("d", k, r, b), X.at[k, r, own(b), scols], X.at[k, r, other(b), scols], partner,
+             recv_ids("d", k, r, b))
 
     def gather_start(k):
         for b in range(2):
-            arrived(X.at[k, 0, own(b)], P1[k][b])
-            send(("u", k, b), X.at[k, 0, own(b)], X.at[k, 3, own(b)], up, recv_ids("u", k, b))
-            send(("n", k, b), X.at[k, 0, own(b)], X.at[k, 1, own(b)], dn, recv_ids("n", k, b))
+            arrived(X.at[k, 0, own(b), scols], P1[k][b])
+            send(("u", k, b), X.at[k, 0, own(b), scols], X.at[k, 3, own(b), scols], up, recv_ids("u", k, b))
+            send(("n", k, b), X.at[k, 0, own(b), scols], X.at[k, 1, own(b), scols], dn, recv_ids("n", k, b))
             to_partner(k, 0, b)
 
     def gather_forward(k):
-        arrived(X.at[k, 3, own(0)], recv_ids("u", k, 0))
-        send(("fu", k), X.at[k, 3, own(0)], X.at[k, 2, own(0)], up, recv_ids("fu", k))
+        arrived(X.at[k, 3, own(0), scols], recv_ids("u", k, 0))
+        send(("fu", k), X.at[k, 3, own(0), scols], X.at[k, 2, own(0), scols], up, recv_ids("fu", k))
         to_partner(k, 3, 0)
-        arrived(X.at[k, 1, own(0)], recv_ids("n", k, 0))
+        arrived(X.at[k, 1, own(0), scols], recv_ids("n", k, 0))
         to_partner(k, 1, 0)
-        arrived(X.at[k, 1, own(1)], recv_ids("n", k, 1))
-        send(("fn", k), X.at[k, 1, own(1)], X.at[k, 2, own(1)], dn, recv_ids("fn", k))
+        arrived(X.at[k, 1, own(1), scols], recv_ids("n", k, 1))
+        send(("fn", k), X.at[k, 1, own(1), scols], X.at[k, 2, own(1), scols], dn, recv_ids("fn", k))
         to_partner(k, 1, 1)
-        arrived(X.at[k, 3, own(1)], recv_ids("u", k, 1))
+        arrived(X.at[k, 3, own(1), scols], recv_ids("u", k, 1))
         to_partner(k, 3, 1)
 
+    def gather_direct(k):
+        for b in range(2):
+            arrived(X.at[k, :, own(b), tcols], P1T[k][b])
+            send(("dt", k, b), X.at[k, :, own(b), tcols], X.at[k, :, other(b), tcols], partner,
+                 recv_ids("dt", k, b))
+
     def gather_end(k):
-        arrived(X.at[k, 2, own(0)], recv_ids("fu", k))
+        arrived(X.at[k, 2, own(0), scols], recv_ids("fu", k))
         to_partner(k, 2, 0)
-        arrived(X.at[k, 2, own(1)], recv_ids("fn", k))
+        arrived(X.at[k, 2, own(1), scols], recv_ids("fn", k))
         to_partner(k, 2, 1)
+        gather_direct(k)
 
     def gathered(k):
         for r in (0, 3, 1, 2):
             for b in range(2):
-                arrived(X.at[k, r, other(b)], recv_ids("d", k, r, b))
+                arrived(X.at[k, r, other(b), scols], recv_ids("d", k, r, b))
+        for b in range(2):
+            arrived(X.at[k, :, other(b), tcols], recv_ids("dt", k, b))
 
     def hidden(k, start, stop):
-        def step(n, carry):
+        def tile(n):
             total = None
             for r in range(4):
                 rows = pl.ds(pl.multiple_of(((y + r) % 4) * QUART, QUART), QUART)
@@ -206,14 +250,21 @@
                 total = term if total is None else total + term
             gate, up_ = total[:, :128], total[:, 128:]
             value = gate / (1.0 + jnp.exp(-gate)) * up_
-            H[:, pl.ds(pl.multiple_of(n * 128, 128), 128)] = value.astype(BF16)
+            first = n * 128 if isinstance(n, int) else pl.multiple_of(n * 128, 128)
+            H[:, pl.ds(first, 128)] = value.astype(BF16)
+
+        def step(i, carry):
+            tile(start + 2 * i)
+            tile(start + 2 * i + 1)
             return carry
 
         if k == 0:
             for n in range(start, stop):
                 for copy in wcopies[n]:
                     copy.wait()
-        lax.fori_loop(start, stop, step, 0)
+        lax.fori_loop(0, (stop - start) // 2, step, 0)
+        if (stop - start) % 2:
+            tile(stop - 1)
 
     def down(k):
         slot = k % 2
@@ -222,41 +273,61 @@
         for r in range(4):
             sent("ds", k - 2, r)
 
-        def step(i, carry):
-            r = 2 - i
-            r = jnp.where(r < 0, 3, r)
+        def quarter(r):
             cols = pl.ds(pl.multiple_of(((y + r) % 4) * QUART, QUART), QUART)
             part = jnp.dot(H[...], wdn[:, cols], preferred_element_type=F32)
             OWN[slot, r] = part[:HALF]
             DS[slot, r] = part[HALF:].astype(BF16)
+
+        def share(r):
+            send(("ds", k, r), DS.at[slot, r], DR.at[k, r], partner, recv_ids("ds", k, r))
+
+        def step(i, carry):
+            quarter(2 + i)
+            quarter(1 - i)
             return carry
 
-        lax.fori_loop(0, 4, step, 0)
-        for r in (2, 1, 3, 0):
-            send(("ds", k, r), DS.at[slot, r], DR.at[k, r], partner, recv_ids("ds", k, r))
-
-    def chip_sum(k, r):
-        arrived(DR.at[k, r], recv_ids("ds", k, r))
-        return OWN[k % 2, r] + DR[k, r].astype(F32)
+        if k < 3:
+            lax.fori_loop(0, 2, step, 0)
+            for r in (2, 1, 3, 0):
+                share(r)
+        else:
+            for r in (2, 1, 3, 0):
+                quarter(r)
+                share(r)
+
+    shared = set()
+
+    def chip_sum(k, r, a, b):
+        if (k, r) not in shared:
+            shared.add((k, r))
+            arrived(DR.at[k, r], recv_ids("ds", k, r))
+        return OWN[k % 2, r, :, a:b] + DR[k, r, :, a:b].astype(F32)
 
     def scatter_start(k):
         slot = k % 2
         sent("a1", k - 2)
         sent("b1", k - 2)
-        T1[slot] = chip_sum(k, 2).astype(BF16)
+        T1[slot] = chip_sum(k, 2, 0, WS).astype(BF16)
         send(("a1", k), T1.at[slot, pl.ds(0, ROWS)], RR1.at[k, 0], dn, recv_ids("a1", k))
         send(("b1", k), T1.at[slot, pl.ds(ROWS, ROWS)], RR1.at[k, 1], up, recv_ids("b1", k))
+        for b in range(2):
+            sent("p3t", k - 2, b)
+        for r in (2, 1, 3, 0):
+            T4[slot, r] = chip_sum(k, r, WS, QUART).astype(BF16)
+        for b in range(2):
+            send(("p3t", k, b), T4.at[slot, :, own(b)], RT.at[k, :, block], sources[k][b], P3T[k][0] + zb)
 
     def scatter_forward(k):
         slot = k % 2
         sent("a2", k - 2)
         sent("b2", k - 2)
-        total = chip_sum(k, 3)
+        total = chip_sum(k, 3, 0, WS)
         arrived(RR1.at[k, 0], recv_ids("a1", k))
         T2[slot, 0, 0:ROWS] = (total[:ROWS] + RR1[k, 0].astype(F32)).astype(BF16)
         T2[slot, 0, ROWS:HALF] = total[ROWS:].astype(BF16)
         send(("a2", k), T2.at[slot, 0], RR2.at[k, 0], dn, recv_ids("a2", k))
-        total = chip_sum(k, 1)
+        total = chip_sum(k, 1, 0, WS)
         arrived(RR1.at[k, 1], recv_ids("b1", k))
         T2[slot, 1, 0:ROWS] = total[:ROWS].astype(BF16)
         T2[slot, 1, ROWS:HALF] = (total[ROWS:] + RR1[k, 1].astype(F32)).astype(BF16)
@@ -266,35 +337,64 @@
         slot = k % 2
         for b in range(2):
             sent("p3", k - 2, b)
-        total = chip_sum(k, 0)
+        total = chip_sum(k, 0, 0, WS)
         arrived(RR2.at[k, 0], recv_ids("a2", k))
         arrived(RR2.at[k, 1], recv_ids("b2", k))
         T3[slot] = (total + RR2[k, 0].astype(F32) + RR2[k, 1].astype(F32)).astype(BF16)
         for b in range(2):
-            send(("p3", k, b), T3.at[slot, own(b)], R.at[k, pl.ds(pl.multiple_of(zb * ROWS, 16), ROWS)],
-                 sources[k][b], P3[k][0] + zb)
+            send(("p3", k, b), T3.at[slot, own(b)], R.at[k, block], sources[k][b], P3[k][0] + zb)
 
     two_lane = lax.broadcasted_iota(jnp.int32, (256, HALF), 1)
     two_lane = jnp.where(two_lane >= ROWS, two_lane - ROWS, two_lane).astype(F32)
+
+    def weights(k):
+        c0, c1 = columns(k)
+        weight = jnp.where(two_lane == c0, w0, 0.0) + jnp.where(two_lane == c1, w1, 0.0)
+        high = weight.astype(BF16)
+        return high, (weight - high.astype(F32)).astype(BF16)
+
+    def mix(high, low, rows):
+        return jnp.dot(high, rows, preferred_element_type=F32) + jnp.dot(
+            low, rows, preferred_element_type=F32
+        )
+
+    def combine_direct(k):
+        for i in range(2):
+            arrived(RT.at[k, :, own(i)], P3T[k][i])
+        high, low = weights(k)
+        for r in range(4):
+            term = mix(high, low, RT[k, r])
+            accT[r] = term if k == 0 else accT[r] + term
 
     def combine(k):
         for i in range(2):
             arrived(R.at[k, own(i)], P3[k][i])
-        c0, c1 = columns(k)
-        weight = jnp.where(two_lane == c0, w0, 0.0) + jnp.where(two_lane == c1, w1, 0.0)
-        high = weight.astype(BF16)
-        low = (weight - high.astype(F32)).astype(BF16)
-        rows = R[k]
-        term = jnp.dot(high, rows, preferred_element_type=F32) + jnp.dot(
-            low, rows, preferred_element_type=F32
-        )
+        high, low = weights(k)
+        term = mix(high, low, R[k])
         acc[...] = term if k == 0 else acc[...] + term
 
+    dispatch(0)
+    dispatch(1)
+    tokens_along_y()
+    dispatch_direct(0)
     gather_start(0)
+    dispatch(2)
+    dispatch(3)
+    dispatch_direct(1)
     gather_start(1)
     gather_forward(0)
+    dispatch_stats()
+    gather_end(0)
+    gathered(0)
+
+    hidden(0, 0, 3)
+    dispatch_direct(2)
+    gather_forward(1)
     gather_start(2)
-    gather_end(0)
+    hidden(0, 3, NT)
+    dispatch_direct(3)
+    gather_end(1)
+    gather_start(3)
     for i in range(8):
         arrived(stat_in.at[i], ST[i])
     total = stat_in[0]
@@ -302,21 +402,15 @@
         total = total + stat_in[i]
     stat_pair[0] = total
     send(("sp",), stat_pair.at[0], stat_pair.at[1], partner, recv_ids("sp"))
-    gathered(0)
-
-    hidden(0, 0, 4)
-    gather_forward(1)
-    gather_start(3)
-    hidden(0, 4, NT)
-    gather_end(1)
     down(0)
+    gather_forward(2)
     gathered(1)
 
     hidden(1, 0, 4)
     scatter_start(0)
-    gather_forward(2)
+    gather_end(2)
     hidden(1, 4, NT)
-    gather_end(2)
+    gather_forward(3)
     scatter_forward(0)
     down(1)
     gathered(2)
@@ -324,34 +418,47 @@
     hidden(2, 0, 4)
     scatter_end(0)
     scatter_start(1)
-    gather_forward(3)
+    gather_end(3)
     hidden(2, 4, NT)
     scatter_forward(1)
-    gather_end(3)
     down(2)
     gathered(3)
 
     hidden(3, 0, 4)
     scatter_end(1)
     scatter_start(2)
+    combine_direct(0)
     hidden(3, 4, NT)
     scatter_forward(2)
     combine(0)
+    combine_direct(1)
     down(3)
 
     scatter_start(3)
     scatter_end(2)
+    combine_direct(2)
     combine(1)
     scatter_forward(3)
+    combine_direct(3)
+    send(("finT",), accT.at[:, theirs], finT_in, partner, recv_ids("finT"))
     arrived(stat_pair.at[1], recv_ids("sp"))
     total = stat_pair[0] + stat_pair[1]
     aux_ref[...] = EXPERTS * (total[0:2, 0:8] / 4096.0) * (total[2:4, 0:8] / 2048.0)
     combine(2)
+    arrived(finT_in, recv_ids("finT"))
+    for r in (2, 1, 3):
+        YS[r] = (accT[r, 0:128] + finT_in[r]).astype(BF16)
+        send(("ys", r), YS.at[r], YR.at[r], round_y[r], recv_ids("ys", r))
     scatter_end(3)
     combine(3)
-    send(("fin",), acc.at[pl.ds(128, 128)], fin_in, partner, recv_ids("fin"))
+    send(("fin",), acc.at[theirs], fin_in, partner, recv_ids("fin"))
+    total = accT[0, 0:128] + finT_in[0]
+    for r in (1, 3, 2):
+        arrived(YR.at[r], recv_ids("ys", r))
+        total = total + YR[r].astype(F32)
+    out_ref[:, WS:QUART] = total.astype(BF16)
     arrived(fin_in, recv_ids("fin"))
-    out_ref[...] = (acc[0:128, :] + fin_in[...]).astype(BF16)
+    out_ref[:, 0:WS] = (acc[0:128, :] + fin_in[...]).astype(BF16)
     for name in list(pending):
         sent(*name)
     assert len(send_ids.names) <= N_SEND and len(recv_ids.names) <= N_RECV
@@ -373,20 +480,29 @@
             pltpu.VMEM((FFD, D), BF16),
             pltpu.VMEM((4, 4, FULL, QUART), BF16),
             pltpu.VMEM((FULL, FFD), BF16),
-            pltpu.VMEM((4, ROWS, QUART), BF16),
+            pltpu.VMEM((4, ROWS, WS), BF16),
+            pltpu.VMEM((4, 4, ROWS, WT), BF16),
             pltpu.VMEM((256, QUART), BF16),
+            pltpu.VMEM((4, 256, WT), BF16),
+            pltpu.VMEM((4, 256, ROWS), BF16),
             pltpu.VMEM((256, 128), F32),
-            pltpu.VMEM((256, QUART), F32),
-            pltpu.VMEM((4, HALF, QUART), BF16),
+            pltpu.VMEM((256, WS), F32),
+            pltpu.VMEM((4, 256, WT), F32),
+            pltpu.VMEM((4, HALF, WS), BF16),
+            pltpu.VMEM((4, 4, HALF, WT), BF16),
             pltpu.VMEM((2, 4, HALF, QUART), BF16),
             pltpu.VMEM((4, 4, HALF, QUART), BF16),
             pltpu.VMEM((2, 4, HALF, QUART), F32),
-            pltpu.VMEM((2, HALF, QUART), BF16),
-            pltpu.VMEM((2, 2, HALF, QUART), BF16),
-            pltpu.VMEM((2, HALF, QUART), BF16),
-            pltpu.VMEM((4, 2, ROWS, QUART), BF16),
-            pltpu.VMEM((4, 2, HALF, QUART), BF16),
-            pltpu.VMEM((128, QUART), F32),
+            pltpu.VMEM((2, HALF, WS), BF16),
+            pltpu.VMEM((2, 2, HALF, WS), BF16),
+            pltpu.VMEM((2, HALF, WS), BF16),
+            pltpu.VMEM((2, 4, HALF, WT), BF16),
+            pltpu.VMEM((4, 2, ROWS, WS), BF16),
+            pltpu.VMEM((4, 2, HALF, WS), BF16),
+            pltpu.VMEM((128, WS), F32),
+            pltpu.VMEM((4, 128, WT), F32),
+            pltpu.VMEM((4, 128, WT), BF16),
+            pltpu.VMEM((4, 128, WT), BF16),
             pltpu.VMEM((8, 128), F32),
             pltpu.VMEM((8, 8, 128), F32),
             pltpu.VMEM((2, 8, 128), F32),

time: 147 us -> 121 us (0.82)
  the two profiles are of different devices: /device:TPU:1 before, /device:TPU:7 now
where the time goes in v2:
time: 121 us
  Pallas kernels  115 us (95%)
  local copies, waits for them, and re-layouts  3.87 us (3%)
  other arithmetic  1.41 us (1%)
    pallas_call x1, Pallas kernels, local(): pl.pallas_call(moe_kernel, out_shape=(jax.ShapeDtypeStruct((128, QUART),...  115 us
    unnamed x3, local copies, waits for them, and re-layouts  3.69 us

profile of v2, /device:TPU:7, one launch (start us, length us, event | category | flops | bytes accessed | tf_op | source)
XLA Modules:
  0.0 120.9 jit_solution(6302993275946331820)
XLA Ops:
  0.6 0.1 pad.2.clone
  0.7 0.7 convert_element_type.6
  1.4 0.1 copy.9
  1.5 0.8 copy.8
  2.3 0.7 maximum_maximum_fusion.meta_ref
  3.0 115.0 %moe.1 = (bf16[128,1024]{1,0:T(8,128)(2,1)}, f32[2,8]{1,0:T(2,128)}) custom-call(bf16[128,1024]{1,0:T(8,128)(2,1)} %bitcast.10, f32[128,128]{1,0:T(8,128)} %maximum_maximum_fusion.meta_ref, bf16[4096,896]{1,0:T(8,128)(2,1)} %bitcast.7, bf16[4096,896]{1,0:T(8,128)(2,1)} %bitcast.8, bf16[896,4096]{1,0:T(8,128)(2,1)} %bitcast.9), custom_call_target="tpu_custom_call" | custom-call | tf_op jit(solution)/shard_map/moe/pallas_call | solution.py:473
  118.0 1.7 %copy.12 = bf16[2,64,1024]{2,1,0:T(8,128)(2,1)} copy(bf16[2,64,1024]{2,1,0:T(8,128)(2,1)} %bitcast.13) | data formatting | bytes 524288
  119.7 1.2 %copy.13 = f32[2,8]{1,0:T(2,128)} copy(f32[2,8]{1,0:T(2,128)} %get-tuple-element.9) | data formatting | bytes 128
  (1 shorter events, 0.0 us)

commit v3 on v2

--- a/solution.py
+++ b/solution.py
@@ -266,7 +266,7 @@
         if (stop - start) % 2:
             tile(stop - 1)
 
-    def down(k):
+    def down(k, between=None):
         slot = k % 2
         if k == 0:
             dcopy.wait()
@@ -295,6 +295,8 @@
             for r in (2, 1, 3, 0):
                 quarter(r)
                 share(r)
+                if r == 1:
+                    between()
 
     shared = set()
 
@@ -311,6 +313,9 @@
         T1[slot] = chip_sum(k, 2, 0, WS).astype(BF16)
         send(("a1", k), T1.at[slot, pl.ds(0, ROWS)], RR1.at[k, 0], dn, recv_ids("a1", k))
         send(("b1", k), T1.at[slot, pl.ds(ROWS, ROWS)], RR1.at[k, 1], up, recv_ids("b1", k))
+
+    def return_direct(k):
+        slot = k % 2
         for b in range(2):
             sent("p3t", k - 2, b)
         for r in (2, 1, 3, 0):
@@ -383,18 +388,19 @@
     dispatch_direct(1)
     gather_start(1)
     gather_forward(0)
+    gather_start(2)
     dispatch_stats()
     gather_end(0)
+    gather_forward(1)
     gathered(0)
 
     hidden(0, 0, 3)
     dispatch_direct(2)
-    gather_forward(1)
-    gather_start(2)
+    gather_start(3)
     hidden(0, 3, NT)
     dispatch_direct(3)
     gather_end(1)
-    gather_start(3)
+    gather_forward(2)
     for i in range(8):
         arrived(stat_in.at[i], ST[i])
     total = stat_in[0]
@@ -403,42 +409,43 @@
     stat_pair[0] = total
     send(("sp",), stat_pair.at[0], stat_pair.at[1], partner, recv_ids("sp"))
     down(0)
-    gather_forward(2)
+    gather_forward(3)
     gathered(1)
 
-    hidden(1, 0, 4)
+    hidden(1, 0, 3)
     scatter_start(0)
+    return_direct(0)
     gather_end(2)
-    hidden(1, 4, NT)
-    gather_forward(3)
+    hidden(1, 3, NT)
     scatter_forward(0)
+    gather_end(3)
     down(1)
     gathered(2)
 
-    hidden(2, 0, 4)
+    hidden(2, 0, 3)
+    scatter_start(1)
+    return_direct(1)
     scatter_end(0)
-    scatter_start(1)
-    gather_end(3)
-    hidden(2, 4, NT)
+    hidden(2, 3, NT)
     scatter_forward(1)
     down(2)
     gathered(3)
 
-    hidden(3, 0, 4)
+    hidden(3, 0, 3)
+    scatter_start(2)
+    return_direct(2)
     scatter_end(1)
-    scatter_start(2)
     combine_direct(0)
-    hidden(3, 4, NT)
+    hidden(3, 3, NT)
     scatter_forward(2)
     combine(0)
     combine_direct(1)
-    down(3)
-
-    scatter_start(3)
+    down(3, lambda: scatter_start(3))
     scatter_end(2)
+    scatter_forward(3)
+    return_direct(3)
     combine_direct(2)
     combine(1)
-    scatter_forward(3)
     combine_direct(3)
     send(("finT",), accT.at[:, theirs], finT_in, partner, recv_ids("finT"))
     arrived(stat_pair.at[1], recv_ids("sp"))

time: 121 us -> 116 us (0.959)
  the two profiles are of different devices: /device:TPU:7 before, /device:TPU:1 now
where the time goes in v3:
time: 116 us; the launch traced here: 115 us
  Pallas kernels  109 us (94%)
  local copies, waits for them, and re-layouts  3.87 us (3%)
  other arithmetic  1.41 us (1%)
    pallas_call x1, Pallas kernels, local(): pl.pallas_call(moe_kernel, out_shape=(jax.ShapeDtypeStruct((128, QUART),...  109 us
    unnamed x3, local copies, waits for them, and re-layouts  3.69 us

profile of v3, /device:TPU:1, one launch (start us, length us, event | category | flops | bytes accessed | tf_op | source)
XLA Modules:
  0.0 115.3 jit_solution(4766888259393811992)
XLA Ops:
  0.6 0.1 pad.2.clone
  0.7 0.7 convert_element_type.6
  1.4 0.1 copy.9
  1.5 0.8 copy.8
  2.3 0.7 maximum_maximum_fusion.meta_ref
  3.0 109.4 %moe.1 = (bf16[128,1024]{1,0:T(8,128)(2,1)}, f32[2,8]{1,0:T(2,128)}) custom-call(bf16[128,1024]{1,0:T(8,128)(2,1)} %bitcast.10, f32[128,128]{1,0:T(8,128)} %maximum_maximum_fusion.meta_ref, bf16[4096,896]{1,0:T(8,128)(2,1)} %bitcast.7, bf16[4096,896]{1,0:T(8,128)(2,1)} %bitcast.8, bf16[896,4096]{1,0:T(8,128)(2,1)} %bitcast.9), custom_call_target="tpu_custom_call" | custom-call | tf_op jit(solution)/shard_map/moe/pallas_call | solution.py:480
  112.4 1.7 %copy.12 = bf16[2,64,1024]{2,1,0:T(8,128)(2,1)} copy(bf16[2,64,1024]{2,1,0:T(8,128)(2,1)} %bitcast.13) | data formatting | bytes 524288
  114.1 1.2 %copy.13 = f32[2,8]{1,0:T(2,128)} copy(f32[2,8]{1,0:T(2,128)} %get-tuple-element.9) | data formatting | bytes 128
  (1 shorter events, 0.0 us)
